TPU v7x, 32 devices: a whole 2x2x4 slice. The times are simulated.
32 devices in a mesh: rows: 32 (over z, y, x, core).
Axes of the slice: x: 2, y: 2, z: 4, core: 2. Of those that a mesh axis runs over, the one named last changes fastest.
Arguments:
- a_mat: float32 [262144, 64], P('rows')
- b_mat: float32 [262144, 4], P('rows')
Outputs:
- output 1: float32 [262144, 64], P('rows')
- output 2: float32 [64, 64], replicated
- output 3: float32 [64, 4], replicated
All inputs are finite; a program needn't handle non-finite values.
Results may differ from a plain program's by a relative error of at most 0.001.
Values sent between devices are 32-bit elements.
A program may use at most 1 GiB of HBM per device.

v0:
```python
import jax
import jax.numpy as jnp
from jax import lax
from jax.sharding import PartitionSpec as P

FULL_PRECISION = lax.Precision.HIGHEST


def solution(mesh):
    def local_fn(a_blk, b_blk):
        rows_local, num_cols = a_blk.shape
        dev_index = lax.axis_index('rows')
        global_row = dev_index * rows_local + jnp.arange(rows_local)
        col_ids = jnp.arange(num_cols)

        def factor_step(col_idx, carry):
            work_mat, reflectors, tau_vec = carry
            column = lax.dynamic_index_in_dim(work_mat, col_idx, axis=1, keepdims=False)
            below_mask = global_row >= col_idx
            at_pivot = global_row == col_idx
            column = jnp.where(below_mask, column, 0.0)
            local_stats = jnp.stack([jnp.sum(column * column), jnp.sum(jnp.where(at_pivot, column, 0.0))])
            col_stats = lax.psum(local_stats, 'rows')
            norm_val = jnp.sqrt(col_stats[0])
            pivot_val = col_stats[1]
            beta_val = jnp.where(pivot_val >= 0.0, -norm_val, norm_val)
            reflector = jnp.where(at_pivot, 1.0, column / (pivot_val - beta_val))
            tau_val = (beta_val - pivot_val) / beta_val
            part_proj = jnp.dot(reflector, work_mat, precision=FULL_PRECISION, preferred_element_type=jnp.float32)
            row_proj = lax.psum(part_proj, 'rows')
            work_mat = work_mat - (tau_val * reflector)[:, None] * row_proj[None, :]
            reflectors = lax.dynamic_update_index_in_dim(reflectors, reflector, col_idx, 0)
            tau_vec = jnp.where(col_ids == col_idx, tau_val, tau_vec)
            return work_mat, reflectors, tau_vec

        init_state = (a_blk, jnp.zeros((num_cols, rows_local), jnp.float32), jnp.zeros((num_cols,), jnp.float32))
        work_mat, reflectors, tau_vec = lax.fori_loop(0, num_cols, factor_step, init_state)
        top_rows = jnp.triu(work_mat[:num_cols])
        r_full = lax.psum(jnp.where(dev_index == 0, top_rows, 0.0), 'rows')

        def form_step(step_idx, q_work):
            col_idx = num_cols - 1 - step_idx
            reflector = lax.dynamic_index_in_dim(reflectors, col_idx, axis=0, keepdims=False)
            tau_val = lax.dynamic_index_in_dim(tau_vec, col_idx, axis=0, keepdims=False)
            part_proj = jnp.dot(reflector, q_work, precision=FULL_PRECISION, preferred_element_type=jnp.float32)
            row_proj = lax.psum(part_proj, 'rows')
            return q_work - (tau_val * reflector)[:, None] * row_proj[None, :]

        eye_part = (global_row[:, None] == col_ids[None, :]).astype(jnp.float32)
        q_work = lax.fori_loop(0, num_cols, form_step, eye_part)
        diag_signs = jnp.sign(jnp.diagonal(r_full))
        q_blk = q_work * diag_signs[None, :]
        r_fac = r_full * diag_signs[:, None]
        part_c = jnp.einsum('rn,rk->nk', q_blk, b_blk, precision=FULL_PRECISION, preferred_element_type=jnp.float32)
        c_mat = lax.psum(part_c, 'rows')
        return q_blk, r_fac, c_mat

    return jax.shard_map(local_fn, mesh=mesh, in_specs=(P('rows', None), P('rows', None)), out_specs=(P('rows', None), P(), P()), check_vma=False)
```

profile of v0, /device:TPU:0, one launch (start us, length us, event | category | flops | bytes accessed | tf_op | source)
XLA Modules:
  0.0 9045.4 jit_solution(15749071122838962302)
XLA Ops:
  2.3 5732.4 %while.34 = (s32[]{:T(128)}, f32[8192,64]{0,1:T(8,128)S(1)}, f32[64,8192]{1,0:T(8,128)}, f32[64]{0:T(128)S(1)}, s32[]{:T(128)}, /*index=5*/s32[]{:T(128)}, f32[]{:T(128)}, s32[]{:T(128)}) while((s32[]{:T(128)}, f32[8192,64]{0,1:T(8,128)S(1)}, f32[64,8192]{1,0:T(8,128)}, f32[64]{0:T(128)S(1)}, s32[]{:T(128)}, /*index=5*/s32[]{:T(128)}, ...), condition=%wide.region_5.6_spmd.clone, body=%wide.region_0.5_spmd.clone.sunk | while | flops 7536907 | bytes 6768417 | solution.py:37
  4.3 41.9 psum.58
  946.1 40.8 psum.59
  1035.7 40.8 psum.59
  1125.2 40.8 psum.59
  1214.7 40.8 psum.59
  1304.3 40.8 psum.59
  1483.3 40.8 psum.59
  1662.4 40.8 psum.59
  1841.5 40.8 psum.59
  2020.6 40.8 psum.59
  2199.6 40.8 psum.59
  2378.7 40.8 psum.59
  2557.8 40.8 psum.59
  2736.9 40.8 psum.59
  2915.9 40.8 psum.59
  3095.0 40.8 psum.59
  3274.1 40.8 psum.59
  3453.2 40.8 psum.59
  3632.2 40.8 psum.59
  3811.3 40.8 psum.59
  3990.4 40.8 psum.59
  4169.5 40.8 psum.59
  4348.5 40.8 psum.59
  4527.6 40.8 psum.59
  4706.7 40.8 psum.59
  4885.8 40.8 psum.59
  5064.8 40.8 psum.59
  5243.9 40.8 psum.59
  5423.0 40.8 psum.59
  5602.1 40.8 psum.59
  5739.8 3213.2 %while.33 = (s32[]{:T(128)}, f32[8192,64]{1,0:T(8,128)}, f32[64]{0:T(128)S(1)}, f32[64,8192]{1,0:T(8,128)}, s32[]{:T(128)}, /*index=5*/s32[]{:T(128)}, s32[]{:T(128)}, s32[]{:T(128)}) while((s32[]{:T(128)}, f32[8192,64]{1,0:T(8,128)}, f32[64]{0:T(128)S(1)}, f32[64,8192]{1,0:T(8,128)}, s32[]{:T(128)}, /*index=5*/s32[]{:T(128)}, s32[]{:T(128)}, ...), condition=%wide.region_8.9_spmd, body=%wide.region_6.8_spmd.sunk | while | flops 7348294 | bytes 6489239 | solution.py:50
  5795.2 40.8 psum.57
  5895.6 40.8 psum.57
  5996.1 40.8 psum.57
  6096.5 40.8 psum.57
  6196.9 40.8 psum.57
  6297.3 40.8 psum.57
  6397.7 40.8 psum.57
  6498.1 40.8 psum.57
  6598.5 40.8 psum.57
  6698.9 40.8 psum.57
  6799.4 40.8 psum.57
  6899.8 40.8 psum.57
  7000.2 40.8 psum.57
  7100.6 40.8 psum.57
  7201.0 40.8 psum.57
  7301.4 40.8 psum.57
  7401.8 40.8 psum.57
  7502.2 40.8 psum.57
  7602.7 40.8 psum.57
  7703.1 40.8 psum.57
  7803.5 40.8 psum.57
  7903.9 40.8 psum.57
  8004.3 40.8 psum.57
  8104.7 40.8 psum.57
  8205.1 40.8 psum.57
  8305.6 40.8 psum.57
  8406.0 40.8 psum.57
  8506.4 40.8 psum.57
  8606.8 40.8 psum.57
  8707.2 40.8 psum.57
  8807.6 40.8 psum.57
  8908.0 40.8 psum.57
  (1240 shorter events, 6336.8 us)
Async XLA Ops:
  0.6 9001.6 %copy-start = (f32[8192,4]{0,1:T(4,128)S(1)}, f32[8192,4]{0,1:T(4,128)}, u32[]{:S(2)}) copy-start(f32[8192,4]{0,1:T(4,128)} %param.7) | copy-start | bytes 393220
  0.6 1.6 copy-start.1
  9002.3 43.2 copy-start.2
where the time goes:
time: 9080 us; the launch traced here: 9050 us
  blocking collectives  7760 us (85%)
  other arithmetic  487 us (5%)
  matrix products  358 us (4%)
  local copies, waits for them, and re-layouts  266 us (3%)
  loops' own time  178 us (2%)
    psum x64, blocking collectives, factor_step(): row_proj = lax.psum(part_proj, 'rows')  2610 us
    psum x64, blocking collectives, form_step(): row_proj = lax.psum(part_proj, 'rows')  2560 us
    psum x64, blocking collectives, factor_step(): col_stats = lax.psum(local_stats, 'rows')  2510 us
    sub x64, other arithmetic, form_step(): return q_work - (tau_val * reflector)[:, None] * row_proj[None, :]  264 us
    dot_general x64, matrix products, form_step(): jnp.dot(reflector, q_work, precision=FULL_PRECISION, preferred_element_ty...  246 us

commit v1 on v0

v1 whole, which is shorter than its diff:
```python
import functools

import jax
import jax.numpy as jnp
from jax import lax
from jax.experimental import pallas as pl
from jax.experimental.pallas import tpu as pltpu
from jax.sharding import PartitionSpec as P

FULL = lax.Precision.HIGHEST
MESH = pl.DeviceIdType.MESH
GROUP = 8
CHUNKS = 8
PIVOT_FLOOR = 1e-6


def dot_nt(a, b):
    return lax.dot_general(a, b, (((1,), (1,)), ((), ())), precision=FULL, preferred_element_type=jnp.float32)


def dot_nn(a, b):
    return lax.dot_general(a, b, (((1,), (0,)), ((), ())), precision=FULL, preferred_element_type=jnp.float32)


def fold(g):
    return jnp.concatenate([g[:32], g[32:]], axis=1)


def unfold_right(p):
    moved = pltpu.roll(p, 64, 1)
    both = jnp.concatenate([moved, p], axis=0)
    rows = lax.broadcasted_iota(jnp.int32, (64, 128), 0)
    cols = lax.broadcasted_iota(jnp.int32, (64, 128), 1)
    return jnp.where(cols < 64, jnp.where(rows == cols, 1.0, 0.0), both)


def factor(w):
    rows = lax.broadcasted_iota(jnp.int32, (64, 128), 0)
    cols = lax.broadcasted_iota(jnp.int32, (64, 128), 1)
    floor = jnp.sum(jnp.where(cols == rows + 64, w, 0.0), axis=1, keepdims=True) * PIVOT_FLOOR
    floor = jnp.broadcast_to(floor, (64, 128))
    row8 = lax.broadcasted_iota(jnp.int32, (8, 128), 0)
    col1 = lax.broadcasted_iota(jnp.int32, (1, 128), 1)
    done = []
    rest = w
    for blk in range(8):
        size = 64 - 8 * blk
        head, tail = rest[:8], (rest[8:] if size > 8 else None)
        lane = 64 + 8 * blk
        head_cols = [jnp.broadcast_to(head[:, lane + j:lane + j + 1], (8, 128)) for j in range(8)]
        tail_cols = None
        if tail is not None:
            tail_cols = [jnp.broadcast_to(tail[:, lane + j:lane + j + 1], (size - 8, 128)) for j in range(8)]
        for k in range(8):
            pivot = head_cols[k][k:k + 1]
            safe = jnp.maximum(pivot, floor[8 * blk + k:8 * blk + k + 1])
            scale = lax.rsqrt(safe)
            row = head[k:k + 1] + jnp.where(col1 == lane + k, safe - pivot, 0.0)
            row = row * scale
            below = jnp.where(row8 > k, head_cols[k] * scale, 0.0)
            head = jnp.where(row8 == k, row, head - below * row)
            if tail is not None:
                tail_k = tail_cols[k] * scale
                tail = tail - tail_k * row
            for j in range(k + 1, 8):
                entry = head_cols[j][k:k + 1] * scale
                head_cols[j] = head_cols[j] - below * entry
                if tail is not None:
                    tail_cols[j] = tail_cols[j] - tail_k * entry
        done.append(head)
        rest = tail
    return jnp.concatenate(done, axis=0)


def upper_of(y):
    moved = pltpu.roll(y, 64, 1)[:, :64]
    rows = lax.broadcasted_iota(jnp.int32, (64, 64), 0)
    cols = lax.broadcasted_iota(jnp.int32, (64, 64), 1)
    return jnp.where(rows <= cols, moved, 0.0)


def tree_sum(ref, count):
    terms = [ref[i] for i in range(count)]
    while len(terms) > 1:
        terms = [terms[i] + terms[i + 1] for i in range(0, len(terms), 2)]
    return terms[0]


def all_sum(part, near, far, near_send, near_recv, far_send, far_recv, devices):
    levels = devices // GROUP
    me = lax.axis_index('rows')
    slot, level = me % GROUP, me // GROUP
    near[slot] = part
    sends = []
    for step in range(GROUP - 1, 0, -1):
        peer = level * GROUP + (slot + step) % GROUP
        copy = pltpu.make_async_remote_copy(
            src_ref=near.at[slot], dst_ref=near.at[slot], send_sem=near_send.at[step], recv_sem=near_recv.at[slot],
            device_id=(peer,), device_id_type=MESH)
        copy.start()
        sends.append(copy)
    for step in range(1, GROUP):
        other = (slot + step) % GROUP
        pltpu.make_async_remote_copy(
            src_ref=near.at[other], dst_ref=near.at[other], send_sem=near_send.at[step], recv_sem=near_recv.at[other],
            device_id=(me,), device_id_type=MESH).wait_recv()
    far[level] = tree_sum(near, GROUP)
    for step in range(levels - 1, 0, -1):
        peer = ((level + step) % levels) * GROUP + slot
        copy = pltpu.make_async_remote_copy(
            src_ref=far.at[level], dst_ref=far.at[level], send_sem=far_send.at[step], recv_sem=far_recv.at[level],
            device_id=(peer,), device_id_type=MESH)
        copy.start()
        sends.append(copy)
    for step in range(1, levels):
        other = (level + step) % levels
        pltpu.make_async_remote_copy(
            src_ref=far.at[other], dst_ref=far.at[other], send_sem=far_send.at[step], recv_sem=far_recv.at[other],
            device_id=(me,), device_id_type=MESH).wait_recv()
    return tree_sum(far, levels), sends


def pass_kernel(devices, a_hbm, b_hbm, q_hbm, p_ref, r_ref, bad_ref, x_ref, b_ref, near1, far1, near2, far2,
                in_sem, b_sem, out_sem, *comm_sems):
    levels = devices // GROUP
    me = lax.axis_index('rows')
    slot, level = me % GROUP, me // GROUP
    rows = a_hbm.shape[1]
    size = rows // CHUNKS

    loads = []
    for i in range(CHUNKS):
        copy = pltpu.make_async_copy(
            a_hbm.at[:, pl.ds(i * size, size)], x_ref.at[pl.ds(0, 64), pl.ds(i * size, size)], in_sem.at[i])
        copy.start()
        loads.append(copy)
    load_b = pltpu.make_async_copy(b_hbm, b_ref, b_sem)
    load_b.start()

    barrier = pltpu.get_barrier_semaphore()
    for step in range(1, GROUP):
        pl.semaphore_signal(barrier, inc=1, device_id=(level * GROUP + (slot + step) % GROUP,), device_id_type=MESH)
    for step in range(1, levels):
        pl.semaphore_signal(barrier, inc=1, device_id=(((level + step) % levels) * GROUP + slot,), device_id_type=MESH)

    gram = jnp.zeros((64, 64), jnp.float32)
    for i in range(CHUNKS):
        loads[i].wait()
        x = x_ref[0:64, i * size:(i + 1) * size]
        gram = gram + dot_nt(x, x)

    pl.semaphore_wait(barrier, GROUP - 1 + levels - 1)
    total, sends = all_sum(fold(gram), near1, far1, *comm_sems[:4], devices)

    load_b.wait()
    y = factor(unfold_right(total))
    inv = y[:, :64]
    r_ref[...] = upper_of(y)

    acc = jnp.zeros((72, 64), jnp.float32)
    stores = []
    for i in range(CHUNKS):
        cols = slice(i * size, (i + 1) * size)
        q = dot_nn(inv, x_ref[0:64, cols])
        x_ref[0:64, cols] = q
        copy = pltpu.make_async_copy(
            x_ref.at[pl.ds(0, 64), pl.ds(i * size, size)], q_hbm.at[:, pl.ds(i * size, size)], out_sem.at[i])
        copy.start()
        stores.append(copy)
        both = jnp.concatenate([q, b_ref[:, cols], jnp.zeros((4, size), jnp.float32)], axis=0)
        acc = acc + dot_nt(both, q)

    part = jnp.concatenate([fold(acc[:64]), jnp.concatenate([acc[64:], jnp.zeros((8, 64), jnp.float32)], axis=1)], axis=0)
    total, more = all_sum(part, near2, far2, *comm_sems[4:], devices)
    p_ref[...] = total

    rows32 = lax.broadcasted_iota(jnp.int32, (32, 128), 0)
    cols32 = lax.broadcasted_iota(jnp.int32, (32, 128), 1)
    eye = jnp.where((cols32 == rows32) | (cols32 == rows32 + 96), 1.0, 0.0)
    off = total[:32] - eye
    bad_ref[...] = jnp.broadcast_to(jnp.sum(off * off), (1, 128))
    for copy in sends + more:
        copy.wait_send()
    for copy in stores:
        copy.wait()


def last_kernel(q1_hbm, p_ref, r1_ref, q_hbm, r_ref, c_ref, x_ref, in_sem, out_sem):
    rows = q1_hbm.shape[1]
    size = rows // CHUNKS
    loads = []
    for i in range(CHUNKS):
        copy = pltpu.make_async_copy(
            q1_hbm.at[:, pl.ds(i * size, size)], x_ref.at[:, pl.ds(i * size, size)], in_sem.at[i])
        copy.start()
        loads.append(copy)
    y = factor(unfold_right(p_ref[0:32, :]))
    inv = y[:, :64]
    stores = []
    for i in range(CHUNKS):
        loads[i].wait()
        cols = slice(i * size, (i + 1) * size)
        x_ref[:, cols] = dot_nn(inv, x_ref[:, cols])
        copy = pltpu.make_async_copy(
            x_ref.at[:, pl.ds(i * size, size)], q_hbm.at[:, pl.ds(i * size, size)], out_sem.at[i])
        copy.start()
        stores.append(copy)
    r_ref[...] = dot_nn(upper_of(y), r1_ref[...])
    c_ref[...] = dot_nt(p_ref[32:40, 0:64], inv)[:4]
    for copy in stores:
        copy.wait()


def solution(mesh):
    devices = mesh.shape['rows']
    levels = devices // GROUP
    any_spec = pl.BlockSpec(memory_space=pl.ANY)
    vmem_spec = pl.BlockSpec(memory_space=pltpu.VMEM)
    f32 = jnp.float32
    dma = pltpu.SemaphoreType.DMA

    def one_pass(x, b):
        rows = x.shape[1]
        return pl.pallas_call(
            functools.partial(pass_kernel, devices),
            out_shape=[
                jax.ShapeDtypeStruct((64, rows), f32), jax.ShapeDtypeStruct((40, 128), f32),
                jax.ShapeDtypeStruct((64, 64), f32), jax.ShapeDtypeStruct((1, 128), f32)],
            in_specs=[any_spec, any_spec],
            out_specs=[any_spec, vmem_spec, vmem_spec, vmem_spec],
            scratch_shapes=[
                pltpu.VMEM((64, rows), f32), pltpu.VMEM((4, rows), f32),
                pltpu.VMEM((GROUP, 32, 128), f32), pltpu.VMEM((levels, 32, 128), f32),
                pltpu.VMEM((GROUP, 40, 128), f32), pltpu.VMEM((levels, 40, 128), f32),
                dma((CHUNKS,)), dma, dma((CHUNKS,)),
                dma((GROUP,)), dma((GROUP,)), dma((levels,)), dma((levels,)),
                dma((GROUP,)), dma((GROUP,)), dma((levels,)), dma((levels,))],
            compiler_params=pltpu.CompilerParams(collective_id=0, has_side_effects=True),
            name='gram_pass',
        )(x, b)

    def last(q1, p, r1):
        rows = q1.shape[1]
        return pl.pallas_call(
            last_kernel,
            out_shape=[
                jax.ShapeDtypeStruct((64, rows), f32), jax.ShapeDtypeStruct((64, 64), f32),
                jax.ShapeDtypeStruct((4, 64), f32)],
            in_specs=[any_spec, vmem_spec, vmem_spec],
            out_specs=[any_spec, vmem_spec, vmem_spec],
            scratch_shapes=[pltpu.VMEM((64, rows), f32), dma((CHUNKS,)), dma((CHUNKS,))],
            name='last_pass',
        )(q1, p, r1)

    def local_fn(a_blk, b_blk):
        b_t = b_blk.T
        q1, p, r1, bad = one_pass(a_blk.T, b_t)

        def again(state):
            q1, p, r1, bad = state
            q2, p, r2, bad = one_pass(q1, b_t)
            return q2, p, jnp.dot(r2, r1, precision=FULL), bad

        q1, p, r1, bad = lax.while_loop(lambda state: state[3][0, 0] > 0.25, again, (q1, p, r1, bad))
        q, r_fac, c = last(q1, p, r1)
        return q.T, r_fac, c.T

    return jax.shard_map(local_fn, mesh=mesh, in_specs=(P('rows', None), P('rows', None)),
                         out_specs=(P('rows', None), P(), P()), check_vma=False)
```

time: 9080 us -> 40.6 us (0.00)
  blocking collectives: 7760 us -> 0 us
  other arithmetic: 487 us -> 0 us
  matrix products: 358 us -> 0 us
  local copies, waits for them, and re-layouts: 266 us -> 0.01 us
  loops' own time: 178 us -> 1.09 us
    psum x194 -> x0, blocking collectives: 7760 us -> none  [the longest x64 2610 us: factor_step(): row_proj = lax.psum(part_proj, 'rows')]
    dot_general x129 -> x0, matrix products: 358 us -> none  [the longest x64 246 us: form_step(): jnp.dot(reflector, q_work, precision=FULL_PRECISION, preferred_element_ty...]
    sub x128 -> x0, other arithmetic: 294 us -> none  [the longest x64 264 us: form_step(): return q_work - (tau_val * reflector)[:, None] * row_proj[None, :]]
    another operation x2 -> x1, loops' own time: 178 us -> 1.09 us  [local_fn(): lax.while_loop(lambda state: state[3][0, 0] > 0.25, again, (q1, p, r1, bad))]
    dynamic_update_slice x64 -> x0, local copies, waits for them, and re-layouts: 113 us -> none  [factor_step(): lax.dynamic_update_index_in_dim(reflectors, reflector, col_idx, 0)]
    dynamic_slice x192 -> x0, local copies, waits for them, and re-layouts: 102 us -> none  [the longest x64 62.3 us: form_step(): lax.dynamic_index_in_dim(reflectors, col_idx, axis=0, keepdims=False)]
where the time goes in v1:
time: 40.6 us; the launch traced here: 40.4 us
  Pallas kernels  38.5 us (95%)
  loops' own time  1.09 us (3%)
  between operations  0.84 us (2%)
    pallas_call x1, Pallas kernels, one_pass(): pl.pallas_call(functools.partial(pass_kernel, devices), out_shape=[jax.Sh...  31.5 us
    pallas_call x1, Pallas kernels, last(): pl.pallas_call(last_kernel, out_shape=[jax.ShapeDtypeStruct((64, rows), f...  6.96 us
    another operation x1, loops' own time, local_fn(): lax.while_loop(lambda state: state[3][0, 0] > 0.25, again, (q1, p, r1, bad))  1.09 us

profile of v1, /device:TPU:0, one launch (start us, length us, event | category | flops | bytes accessed | tf_op | source)
XLA Modules:
  0.0 40.4 jit_solution(11409610076204804515)
XLA Ops:
  0.6 0.0 copy-start
  0.6 31.5 %gram_pass.3 = (f32[64,8192]{1,0:T(8,128)S(1)}, f32[40,128]{1,0:T(8,128)}, f32[64,64]{1,0:T(8,128)S(1)}, f32[1,128]{1,0:T(1,128)}) custom-call(f32[64,8192]{1,0:T(8,128)} %bitcast.10, f32[4,8192]{1,0:T(4,128)} %bitcast.8), custom_call_target="tpu_custom_call" | custom-call | tf_op jit(solution)/shard_map/gram_pass/pallas_call | solution.py:224
  32.2 0.0 copy-done
  32.2 1.1 %while.13 = (f32[64,8192]{1,0:T(8,128)S(1)}, f32[40,128]{1,0:T(8,128)}, f32[64,64]{1,0:T(8,128)S(1)}, f32[1,128]{1,0:T(1,128)}, f32[4,8192]{1,0:T(4,128)S(1)}) while((f32[64,8192]{1,0:T(8,128)S(1)}, f32[40,128]{1,0:T(8,128)}, f32[64,64]{1,0:T(8,128)S(1)}, f32[1,128]{1,0:T(1,128)}, f32[4,8192]{1,0:T(4,128)S(1)}) %tuple.20), condition=%region_1.0_spmd, body=%region_0.0_spmd | while | flops 3145729 | bytes 4276273 | solution.py:264
  33.3 7.0 %last_pass.1 = (f32[64,8192]{1,0:T(8,128)}, f32[64,64]{1,0:T(8,128)}, f32[4,64]{1,0:T(4,128)}) custom-call(f32[64,8192]{1,0:T(8,128)S(1)} %get-tuple-element.45.q1_hbm, f32[40,128]{1,0:T(8,128)} %get-tuple-element.46.p_ref, f32[64,64]{1,0:T(8,128)S(1)} %get-tuple-element.47.r1_ref), custom_call_target="tpu_custom_call" | custom-call | tf_op jit(solution)/shard_map/last_pass/pallas_call | solution.py:244
Async XLA Ops:
  0.6 31.5 %copy-start = (f32[8192,4]{0,1:T(4,128)S(1)}, f32[8192,4]{0,1:T(4,128)}, u32[]{:S(2)}) copy-start(f32[8192,4]{0,1:T(4,128)} %param.5) | copy-start | bytes 393220
